TPU v7x, 32 devices: a whole 2x2x4 slice. The times are simulated.
32 devices in a mesh: grp: 4 (over y, core), sp: 8 (over z, x).
Axes of the slice: x: 2, y: 2, z: 4, core: 2. Of those that a mesh axis runs over, the one named last changes fastest.
Arguments:
- bucket_of: int32 [4], replicated, may hold values from 0 to 3, as said below
- lengths: int32 [4], replicated, may hold values from 128 to 512, as said below
- counts: int32 [4], replicated, may hold values from 256 to 4096
- queries: bfloat16 [4096, 4096], P(('grp', 'sp')), may hold values from -4.5 to 4.5
- keys: bfloat16 [4096, 4096], P(('grp', 'sp')), may hold values from -4.5 to 4.5
- values: bfloat16 [4096, 4096], P(('grp', 'sp')), may hold values from -6 to 6
- out_grad: bfloat16 [4096, 3072], P(('grp', 'sp')), may hold values from -6 to 6
- w_out: bfloat16 [4096, 3072], P('sp', 'grp'), may hold values from -1.75 to 1.75
Outputs:
- grad_queries: bfloat16 [4096, 4096], P(('grp', 'sp'))
- grad_keys: bfloat16 [4096, 4096], P(('grp', 'sp'))
- grad_values: bfloat16 [4096, 4096], P(('grp', 'sp'))
- grad_w_out: float32 [4096, 3072], P('sp', 'grp')
Inputs may be any that keep to these rules, and one draw needn't show every extreme that they name: `bucket_of`: every one of the 4 buckets is held by at least one group. `lengths`: one bucket has length exactly 512.
All inputs are finite; a program needn't handle non-finite values.
Results may differ from a plain program's by a relative error of at most 0.0091.
Values may be sent and summed in bfloat16 or wider, within the bound.
A program may use at most 128 MiB of HBM per device.

v0:
```python
import functools

import jax
import jax.numpy as jnp
from jax import lax
from jax.experimental import pallas as pl
from jax.experimental.pallas import tpu as pltpu
from jax.sharding import PartitionSpec as P

HEAD_DIM = 128
SEQS = 2
MESH = pl.DeviceIdType.MESH
F32 = jnp.float32
BF16 = jnp.bfloat16


def dot(a, b, ca, cb):
    return lax.dot_general(a, b, (((ca,), (cb,)), ((), ())), preferred_element_type=F32)


def kernel(
    G, S, D, W,
    bucket_ref, length_ref, count_ref, q_ref, k_ref, v_ref, og_ref, w_ref,
    gq_ref, gk_ref, gv_ref, gw_ref,
    qh, kh, vh, dqs, dks, dvs, og, w, d_attn, attn_t, gs1, gr1, gown, gs2, gr2, gkeep, gs3, gr3,
    og_s, og_r, oz_s, oz_r, or_s, or_r, og_l, x_s, x_r, x_l, b_s, b_r, b_l,
    w0_s, w0_r, w_l, wy_s, wy_r, ws_s, ws_r, g1_s, g1_r, g2_s, g2_r, g3_s, g3_r,
):
    J = S // SEQS
    H = G // 2
    T = q_ref.shape[0]
    HD = q_ref.shape[1]
    L = J * T
    R = HD // S
    NCH = SEQS * R // W
    NH2 = NCH // 2
    Dc = D // G
    scale = HEAD_DIM ** (-0.5)

    g = lax.axis_index("grp")
    s = lax.axis_index("sp")
    u, j = s // J, s % J
    h, c = g // 2, g % 2
    partner = (g, (1 - u) * J + j)
    sibling = (h * 2 + 1 - c, s)

    def to_h(e):
        return ((h + e) % H * 2 + c, s)

    def seq_peer(d):
        return (g, u * J + (j + d) % J)

    peers = [seq_peer(d) for d in range(1, J)] + [to_h(e) for e in range(1, H)] + [partner, sibling]
    barrier = pltpu.get_barrier_semaphore()
    for peer in peers:
        pl.semaphore_signal(barrier, inc=1, device_id=peer, device_id_type=MESH)
    pl.semaphore_wait(barrier, len(peers))

    def remote(src, dst, ss, rs, dev):
        return pltpu.make_async_remote_copy(
            src_ref=src, dst_ref=dst, send_sem=ss, recv_sem=rs, device_id=dev, device_id_type=MESH
        )

    def half_of(ch):
        return (ch // NH2 + 1 + u) % 2

    def col_of(ch, jj):
        return pl.multiple_of(half_of(ch) * (J * R) + jj * R + ch % NH2 * W, W)

    def rows(jj):
        return pl.ds(pl.multiple_of(jj * T, T), T)

    xs = ((q_ref, qh), (k_ref, kh), (v_ref, vh))
    bs = ((dqs, gq_ref), (dks, gk_ref), (dvs, gv_ref))

    def w0_copy(ch):
        return remote(
            w_ref.at[pl.ds(ch * W, W)], w.at[ch, g], w0_s.at[ch], w0_r.at[ch], partner
        )

    def w_own(ch):
        return w_ref.at[pl.ds((ch - NH2) * W, W)] if ch >= NH2 else w.at[ch, g]

    def wy_copy(ch, e):
        return remote(w_own(ch), w.at[ch, g], wy_s.at[ch, e], wy_r.at[ch, e], to_h(e))

    def ws_copy(ch, e):
        if e == 0:
            return remote(w_own(ch), w.at[ch, g], ws_s.at[ch, 0], ws_r.at[ch, 0], sibling)
        src = (h - e + H) % H * 2 + c
        return remote(w.at[ch, src], w.at[ch, src], ws_s.at[ch, e], ws_r.at[ch, e], sibling)

    def wy_arrival(ch, e):
        src = (h - e + H) % H * 2 + c
        return remote(w.at[ch, src], w.at[ch, src], wy_s.at[ch, e], wy_r.at[ch, e], to_h(e))

    def ws_arrival(ch, e):
        src = (h - e + H) % H * 2 + 1 - c
        return remote(w.at[ch, src], w.at[ch, src], ws_s.at[ch, e], ws_r.at[ch, e], sibling)

    X = J // 2
    jz, jx = j // X, j % X
    mate = (1 - jz) * X + jx

    def og_x_peer(e):
        return (g, u * J + jz * X + (jx + e) % X)

    def piece(jj, p):
        return og.at[pl.ds(pl.multiple_of(jj * T + p * (T // 2), T // 2), T // 2)]

    def og_z(p):
        src = og_ref.at[pl.ds(p * (T // 2), T // 2)]
        return remote(src, piece(j, p), oz_s.at[p], oz_r.at[p], (g, u * J + mate))

    def og_z_arrival(p):
        src = og_ref.at[pl.ds(p * (T // 2), T // 2)]
        return remote(src, piece(mate, p), oz_s.at[p], oz_r.at[p], (g, u * J + mate))

    def og_x(e):
        return remote(og_ref, og.at[rows(j)], og_s.at[e], og_r.at[e], og_x_peer(e))

    def og_x_arrival(e):
        src = rows(jz * X + (jx - e + X) % X)
        return remote(og_ref, og.at[src], og_s.at[e], og_r.at[e], og_x_peer(e))

    def og_relay(e, p):
        block = piece(mate, p)
        return remote(block, block, or_s.at[e, p], or_r.at[e, p], og_x_peer(e))

    def og_relay_arrival(e, p):
        block = piece((1 - jz) * X + (jx - e + X) % X, p)
        return remote(block, block, or_s.at[e, p], or_r.at[e, p], og_x_peer(e))

    def x_copy(ch, i, d):
        src, dst = xs[i]
        cols = pl.ds(col_of(ch, (j + d) % J), W)
        return remote(
            src.at[:, cols], dst.at[ch, rows(j)], x_s.at[ch, i, d], x_r.at[ch, i, d], seq_peer(d)
        )

    def x_arrival(ch, i, d):
        src, dst = xs[i]
        return remote(
            src.at[:, pl.ds(0, W)], dst.at[ch, rows((j - d + J) % J)],
            x_s.at[ch, i, d], x_r.at[ch, i, d], seq_peer(d),
        )

    def x_local(ch, i):
        src, dst = xs[i]
        return pltpu.make_async_copy(
            src.at[:, pl.ds(col_of(ch, j), W)], dst.at[ch, rows(j)], x_l.at[ch, i]
        )

    def b_copy(ch, i, d):
        src, dst = bs[i]
        return remote(
            src.at[ch, rows((j + d) % J)], dst.at[:, pl.ds(col_of(ch, j), W)],
            b_s.at[ch, i, d], b_r.at[ch, i, d], seq_peer(d),
        )

    def b_arrival(ch, i, d):
        src, dst = bs[i]
        return remote(
            src.at[ch, rows(j)], dst.at[:, pl.ds(col_of(ch, (j - d + J) % J), W)],
            b_s.at[ch, i, d], b_r.at[ch, i, d], seq_peer(d),
        )

    def b_local(ch, i):
        src, dst = bs[i]
        return pltpu.make_async_copy(
            src.at[ch, rows(j)], dst.at[:, pl.ds(col_of(ch, j), W)], b_l.at[ch, i]
        )

    og_own = pltpu.make_async_copy(og_ref, og.at[rows(j)], og_l)

    def w_local(ch):
        return pltpu.make_async_copy(w_own(ch), w.at[ch, g], w_l.at[ch])

    def g1_copy(ch):
        return remote(gs1.at[ch], gr1.at[ch], g1_s.at[ch], g1_r.at[ch], sibling)

    def g2_copy(ch, e):
        return remote(gs2.at[ch, e], gr2.at[ch, e], g2_s.at[ch, e], g2_r.at[ch, e], to_h(e))

    def g3_copy(ch):
        return remote(gs3.at[ch], gr3.at[ch], g3_s.at[ch], g3_r.at[ch], partner)

    w0_copy(0).start()
    og_z(0).start()
    og_z(1).start()
    for ch in range(1, NH2):
        w0_copy(ch).start()
    for e in range(1, X):
        og_x(e).start()
    for ch in range(NH2, NCH):
        for e in range(1, H):
            wy_copy(ch, e).start()
        ws_copy(ch, 0).start()
        w_local(ch).start()
    og_own.start()

    def send_chunk(ch, carry):
        for i in range(3):
            for d in range(1, J):
                x_copy(ch, i, d).start()
            x_local(ch, i).start()
        return carry

    send_chunk(0, 0)

    def relay_w0(ch):
        w0_copy(ch).wait_recv()
        for e in range(1, H):
            wy_copy(ch, e).start()
        ws_copy(ch, 0).start()

    relay_w0(0)
    for p in range(2):
        og_z_arrival(p).wait_recv()
        for e in range(1, X):
            og_relay(e, p).start()
    lax.fori_loop(1, NCH, send_chunk, 0)
    for ch in range(1, NH2):
        relay_w0(ch)
    for ch in list(range(NH2, NCH)) + list(range(NH2)):
        for e in range(1, H):
            wy_arrival(ch, e).wait_recv()
            ws_copy(ch, e).start()
    for ch in range(NH2, NCH):
        w_local(ch).wait()
    og_own.wait()
    for e in range(1, X):
        og_x_arrival(e).wait_recv()
        og_relay_arrival(e, 0).wait_recv()
        og_relay_arrival(e, 1).wait_recv()

    seq_len = length_ref[bucket_ref[g]]
    total = count_ref[bucket_ref[0]]
    for other in range(1, G):
        total = total + count_ref[bucket_ref[other]]
    weight = jnp.full((1, 1), count_ref[bucket_ref[g]], jnp.int32).astype(F32) / jnp.full(
        (1, 1), total, jnp.int32
    ).astype(F32)
    keep_key = lax.broadcasted_iota(jnp.int32, (L, 1), 0) < seq_len
    keep_col = lax.broadcasted_iota(jnp.int32, (1, L), 1) < seq_len

    def compute(ch):
        for i in range(3):
            x_local(ch, i).wait()
            for d in range(1, J):
                x_arrival(ch, i, d).wait_recv()
        for e in range(H):
            ws_arrival(ch, e).wait_recv()
        acc = dot(og[:, 0:Dc], w[ch, 0], 1, 1)
        for gg in range(1, G):
            acc = acc + dot(og[:, gg * Dc:(gg + 1) * Dc], w[ch, gg], 1, 1)
        d_attn[...] = jnp.where(keep_key, acc, 0.0).astype(BF16)

        for n in range(W // HEAD_DIM):
            lanes = slice(n * HEAD_DIM, (n + 1) * HEAD_DIM)
            q = qh[ch, :, lanes]
            k = kh[ch, :, lanes]
            v = vh[ch, :, lanes]
            do = d_attn[:, lanes]
            scores = jnp.where(keep_key, dot(k, q, 1, 1) * scale, -1e30)
            top = jnp.max(scores, axis=0, keepdims=True)
            ex = jnp.exp(scores - top)
            probs = ex * (1.0 / jnp.sum(ex, axis=0, keepdims=True))
            low = probs.astype(BF16)
            attn = dot(v, low, 0, 0)
            attn_t[lanes, :] = jnp.where(keep_col, attn, 0.0).astype(BF16)
            dp = dot(v, do, 1, 1)
            delta = jnp.sum(probs * dp, axis=0, keepdims=True)
            ds = (probs * (dp - delta)).astype(BF16)
            dvs[ch, :, lanes] = dot(low, do, 1, 0).astype(BF16)
            dks[ch, :, lanes] = (dot(ds, q, 1, 0) * scale).astype(BF16)
            dqs[ch, :, lanes] = (dot(k, ds, 0, 0) * scale).T.astype(BF16)
        for i in range(3):
            for d in range(1, J):
                b_copy(ch, i, d).start()
            b_local(ch, i).start()
        for hh in range(H):
            low_c, high_c = (
                dot(attn_t[...], og[:, gg * Dc:(gg + 1) * Dc], 1, 0) * weight
                for gg in (2 * hh, 2 * hh + 1)
            )
            gown[ch, hh] = jnp.where(c == 0, low_c, high_c)
            gs1[ch, hh] = jnp.where(c == 0, high_c, low_c).astype(BF16)
        g1_copy(ch).start()

    def across_groups(ch):
        g1_copy(ch).wait_recv()
        for e in range(1, H):
            to = (h + e) % H
            gs2[ch, e] = (gown[ch, to] + gr1[ch, to].astype(F32)).astype(BF16)
            g2_copy(ch, e).start()
        gkeep[ch] = gown[ch, h] + gr1[ch, h].astype(F32)

    def across_halves(ch):
        part = gkeep[ch]
        for e in range(1, H):
            g2_copy(ch, e).wait_recv()
            part = part + gr2[ch, e].astype(F32)

        @pl.when(ch < NH2)
        def _():
            gs3[ch] = part.astype(BF16)
            g3_copy(ch).start()

        @pl.when(ch >= NH2)
        def _():
            gkeep[ch] = part

    def step(n, carry):
        @pl.when(n < NCH)
        def _():
            compute(n)

        @pl.when((n >= 1) & (n < NCH + 1))
        def _():
            across_groups(n - 1)

        @pl.when(n >= 2)
        def _():
            across_halves(n - 2)

        return carry

    lax.fori_loop(0, NCH + 2, step, 0)

    for ch in range(NH2):
        g3_copy(ch).wait_recv()
        gw_ref[ch * W:(ch + 1) * W, :] = gkeep[NH2 + ch] + gr3[ch].astype(F32)

    og_z(0).wait_send()
    og_z(1).wait_send()
    for e in range(1, X):
        og_x(e).wait_send()
        og_relay(e, 0).wait_send()
        og_relay(e, 1).wait_send()
    for ch in range(NCH):
        if ch < NH2:
            w0_copy(ch).wait_send()
            g3_copy(ch).wait_send()
        for e in range(H):
            ws_copy(ch, e).wait_send()
        for e in range(1, H):
            wy_copy(ch, e).wait_send()
            g2_copy(ch, e).wait_send()
        g1_copy(ch).wait_send()

    def drain(ch, carry):
        for i in range(3):
            b_local(ch, i).wait()
            for d in range(1, J):
                x_copy(ch, i, d).wait_send()
                b_copy(ch, i, d).wait_send()
                b_arrival(ch, i, d).wait_recv()
        return carry

    lax.fori_loop(0, NCH, drain, 0)


def solution(mesh):
    G, S = mesh.shape["grp"], mesh.shape["sp"]
    J, H = S // SEQS, G // 2
    X = J // 2

    def shards(bucket_of, lengths, counts, queries, keys, values, out_grad, w_out):
        T, HD = queries.shape
        D = out_grad.shape[1]
        L, R, Dc = J * T, HD // S, D // G
        W = 256 if R % 256 == 0 else 128
        NCH = SEQS * R // W
        NH2 = NCH // 2
        dma = pltpu.SemaphoreType.DMA
        head = pltpu.VMEM((NCH, L, W), BF16)
        smem = pl.BlockSpec(memory_space=pltpu.SMEM)
        hbm = pl.BlockSpec(memory_space=pltpu.HBM)
        grad = jax.ShapeDtypeStruct((T, HD), BF16)
        return pl.pallas_call(
            functools.partial(kernel, G, S, D, W),
            out_shape=(grad, grad, grad, jax.ShapeDtypeStruct((R, Dc), F32)),
            in_specs=[smem] * 3 + [hbm] * 5,
            out_specs=(hbm, hbm, hbm, pl.BlockSpec(memory_space=pltpu.VMEM)),
            scratch_shapes=[head] * 6 + [
                pltpu.VMEM((L, D), BF16),
                pltpu.VMEM((NCH, G, W, Dc), BF16),
                pltpu.VMEM((L, W), BF16),
                pltpu.VMEM((W, L), BF16),
                pltpu.VMEM((NCH, H, W, Dc), BF16),
                pltpu.VMEM((NCH, H, W, Dc), BF16),
                pltpu.VMEM((NCH, H, W, Dc), F32),
                pltpu.VMEM((NCH, H, W, Dc), BF16),
                pltpu.VMEM((NCH, H, W, Dc), BF16),
                pltpu.VMEM((NCH, W, Dc), F32),
                pltpu.VMEM((NH2, W, Dc), BF16),
                pltpu.VMEM((NH2, W, Dc), BF16),
                dma((X,)), dma((X,)), dma((2,)), dma((2,)), dma((X, 2)), dma((X, 2)), dma(()),
                dma((NCH, 3, J)), dma((NCH, 3, J)), dma((NCH, 3)),
                dma((NCH, 3, J)), dma((NCH, 3, J)), dma((NCH, 3)),
                dma((NH2,)), dma((NH2,)), dma((NCH,)),
                dma((NCH, H)), dma((NCH, H)), dma((NCH, H)), dma((NCH, H)),
                dma((NCH,)), dma((NCH,)), dma((NCH, H)), dma((NCH, H)),
                dma((NH2,)), dma((NH2,)),
            ],
            compiler_params=pltpu.CompilerParams(
                collective_id=0, has_side_effects=True, vmem_limit_bytes=62 * 1024 * 1024
            ),
        )(bucket_of, lengths, counts, queries, keys, values, out_grad, w_out)

    rows = P(("grp", "sp"), None)
    return jax.shard_map(
        shards,
        mesh=mesh,
        in_specs=(P(), P(), P(), rows, rows, rows, rows, P("sp", "grp")),
        out_specs=(rows, rows, rows, P("sp", "grp")),
        check_vma=False,
    )
```

profile of v0, /device:TPU:0, one launch (start us, length us, event | category | flops | bytes accessed | tf_op | source)
XLA Modules:
  0.0 135.3 jit_solution(5039244806698533814)
XLA Ops:
  0.6 129.1 %shard_map.111 = (bf16[128,4096]{1,0:T(8,128)(2,1)}, bf16[128,4096]{1,0:T(8,128)(2,1)}, bf16[128,4096]{1,0:T(8,128)(2,1)}, f32[512,768]{1,0:T(8,128)}) custom-call(s32[4]{0:T(128)} %bucket_ref.1, s32[4]{0:T(128)} %length_ref.1, s32[4]{0:T(128)} %count_ref.1, bf16[128,4096]{1,0:T(8,128)(2,1)} %q_ref.1, bf16[128,4096]{1,0:T(8,128)(2,1)} %k_ref.1, ...), custom_call_target="tpu_custom_call" | custom-call | tf_op jit(solution)/shard_map/pallas_call | solution.py:381
  129.8 0.0 copy-start.2
  129.8 0.0 copy-start.1
  129.8 2.4 %copy.16 = bf16[128,4096]{1,0:T(8,128)(2,1)} copy(bf16[128,4096]{1,0:T(8,128)(2,1)} %get-tuple-element.8) | data formatting | bytes 2097152
  132.2 0.0 copy-done.2
  132.2 0.0 copy-start
  132.2 1.0 copy.17
  133.2 0.0 copy-done.1
  133.2 1.0 copy.18
  134.2 0.0 copy-done
  134.2 1.1 copy.19
Async XLA Ops:
  129.8 2.5 %copy-start.2 = (bf16[128,4096]{1,0:T(8,128)(2,1)S(1)}, bf16[128,4096]{1,0:T(8,128)(2,1)}, u32[]{:S(2)}) copy-start(bf16[128,4096]{1,0:T(8,128)(2,1)} %get-tuple-element.9) | copy-start | bytes 3145732
  129.8 3.4 %copy-start.1 = (bf16[128,4096]{1,0:T(8,128)(2,1)S(1)}, bf16[128,4096]{1,0:T(8,128)(2,1)}, u32[]{:S(2)}) copy-start(bf16[128,4096]{1,0:T(8,128)(2,1)} %get-tuple-element.10) | copy-start | bytes 3145732
  132.2 1.9 %copy-start = (f32[512,768]{1,0:T(8,128)S(1)}, f32[512,768]{1,0:T(8,128)}, u32[]{:S(2)}) copy-start(f32[512,768]{1,0:T(8,128)} %get-tuple-element.11) | copy-start | bytes 4718596
where the time goes:
time: 135 us
  Pallas kernels  129 us (96%)
  local copies, waits for them, and re-layouts  5.53 us (4%)
    pallas_call x1, Pallas kernels, shards(): pl.pallas_call(functools.partial(kernel, G, S, D, W), out_shape=(grad, gr...  129 us
    unnamed x10, local copies, waits for them, and re-layouts  5.53 us

commit v1 on v0

v1 whole, which is shorter than its diff:
```python
import functools

import jax
import jax.numpy as jnp
from jax import lax
from jax.experimental import pallas as pl
from jax.experimental.pallas import tpu as pltpu
from jax.sharding import PartitionSpec as P

HEAD_DIM = 128
SEQS = 2
LAG = 2
MESH = pl.DeviceIdType.MESH
F32 = jnp.float32
BF16 = jnp.bfloat16


def dot(a, b, ca, cb):
    return lax.dot_general(a, b, (((ca,), (cb,)), ((), ())), preferred_element_type=F32)


def kernel(
    G, S, D, W, E,
    bucket_ref, length_ref, count_ref, q_ref, k_ref, v_ref, og_ref, w_ref,
    gq_ref, gk_ref, gv_ref, gw_ref,
    qh, kh, vh, dqs, dks, dvs, og, w, d_attn, attn_t, gs1, gr1, gown, gs2, gr2, gkeep, gs3, gr3,
    og_s, og_r, oz_s, oz_r, or_s, or_r, og_l, x_s, x_r, x_l, b_s, b_r, b_l,
    w0_s, w0_r, w_l, wy_s, wy_r, ws_s, ws_r, g1_s, g1_r, g2_s, g2_r, g3_s, g3_r,
):
    J = S // SEQS
    X = J // 2
    H = G // 2
    T = q_ref.shape[0]
    HD = q_ref.shape[1]
    L = J * T
    O = HD // S // W
    FM = 2 * O - E
    NM = FM + O
    NEAR = O - E
    BIG = 4 * O
    Dc = D // G
    scale = HEAD_DIM ** (-0.5)

    g = lax.axis_index("grp")
    s = lax.axis_index("sp")
    z, jx = s // X, s % X
    u, jz = z // 2, z % 2
    mid = (u + jz) % 2
    j = jz * X + jx
    h, c = g // 2, g % 2
    sibling = (h * 2 + 1 - c, s)

    def at(uu, mm, x):
        return (uu * 2 + (uu + mm) % 2) * X + x

    def foreign_of(mm):
        return E + mm * (FM - E)

    foreign = foreign_of(mid)
    mine = foreign + O
    theirs = foreign_of(1 - mid) + O

    def foreign_source(n, mm):
        far = mm * ((n + BIG - NEAR) // BIG)
        return 1 - far, n + mm * ((1 - far) * E - far * NEAR)

    def to_h(e):
        return ((h + e) % H * 2 + c, s)

    def seq_x(d):
        return (jx + d % X) % X

    def seq_from_x(d):
        return (jx - d % X + X) % X

    def seq_mid(d):
        return (mid + d // X) % 2

    def seq_row(d, x):
        return (jz + d // X) % 2 * X + x

    def seq_peer(d):
        return (g, at(u, seq_mid(d), seq_x(d)))

    across_mid = (g, at(1 - u, 1, jx))
    across_edge = (g, at(1 - u, 0, jx))

    peers = [seq_peer(d) for d in range(1, J)] + [to_h(e) for e in range(1, H)] + [sibling, across_mid]
    barrier = pltpu.get_barrier_semaphore()
    for peer in peers:
        pl.semaphore_signal(barrier, inc=1, device_id=peer, device_id_type=MESH)

    @pl.when(mid == 1)
    def _():
        pl.semaphore_signal(barrier, inc=1, device_id=across_edge, device_id_type=MESH)

    pl.semaphore_wait(barrier, len(peers) + mid)

    def remote(src, dst, ss, rs, dev):
        return pltpu.make_async_remote_copy(
            src_ref=src, dst_ref=dst, send_sem=ss, recv_sem=rs, device_id=dev, device_id_type=MESH
        )

    def col_of(ch, mm, x):
        first = foreign_of(mm)
        own = (ch + BIG - first) // BIG
        source_mid, piece_at = foreign_source(ch, mm)
        source = own * at(u, mm, x) + (1 - own) * at(1 - u, source_mid, x)
        return pl.multiple_of((source * O + own * (ch - first) + (1 - own) * piece_at) * W, W)

    def rows(jj):
        return pl.ds(pl.multiple_of(jj * T, T), T)

    xs = ((q_ref, qh), (k_ref, kh), (v_ref, vh))
    bs = ((dqs, gq_ref), (dks, gk_ref), (dvs, gv_ref))

    def w_rows(m):
        return w_ref.at[pl.ds(m * W, W)]

    def w0_copy(m):
        target_mid, n = (1 - mid, m) if m < E else (1, m - E)
        n = (1 - mid) * (NEAR + m) + mid * n
        return remote(w_rows(m), w.at[n, g], w0_s.at[m], w0_r.at[n], (g, at(1 - u, target_mid, jx)))

    def w0_arrival(n):
        return remote(w.at[n, g], w.at[n, g], w0_s.at[0], w0_r.at[n], across_mid)

    def wy_copy(src, ch, e):
        return remote(src, w.at[ch, g], wy_s.at[ch, e], wy_r.at[ch, e], to_h(e))

    def ws_own(src, ch):
        return remote(src, w.at[ch, g], ws_s.at[ch, 0], ws_r.at[ch, 0], sibling)

    def ws_copy(ch, e):
        src = (h - e + H) % H * 2 + c
        return remote(w.at[ch, src], w.at[ch, src], ws_s.at[ch, e], ws_r.at[ch, e], sibling)

    def wy_arrival(ch, e):
        src = (h - e + H) % H * 2 + c
        return remote(w.at[ch, src], w.at[ch, src], wy_s.at[ch, e], wy_r.at[ch, e], to_h(e))

    def ws_arrival(ch, e):
        src = (h - e + H) % H * 2 + 1 - c
        return remote(w.at[ch, src], w.at[ch, src], ws_s.at[ch, e], ws_r.at[ch, e], sibling)

    mate = (1 - jz) * X + jx

    def og_x_peer(e):
        return (g, u * J + jz * X + (jx + e) % X)

    def piece(jj, p):
        return og.at[pl.ds(pl.multiple_of(jj * T + p * (T // 2), T // 2), T // 2)]

    def og_z(p):
        src = og_ref.at[pl.ds(p * (T // 2), T // 2)]
        return remote(src, piece(j, p), oz_s.at[p], oz_r.at[p], (g, u * J + mate))

    def og_z_arrival(p):
        src = og_ref.at[pl.ds(p * (T // 2), T // 2)]
        return remote(src, piece(mate, p), oz_s.at[p], oz_r.at[p], (g, u * J + mate))

    def og_x(e):
        return remote(og_ref, og.at[rows(j)], og_s.at[e], og_r.at[e], og_x_peer(e))

    def og_x_arrival(e):
        src = rows(jz * X + (jx - e + X) % X)
        return remote(og_ref, og.at[src], og_s.at[e], og_r.at[e], og_x_peer(e))

    def og_relay(e, p):
        block = piece(mate, p)
        return remote(block, block, or_s.at[e, p], or_r.at[e, p], og_x_peer(e))

    def og_relay_arrival(e, p):
        block = piece((1 - jz) * X + (jx - e + X) % X, p)
        return remote(block, block, or_s.at[e, p], or_r.at[e, p], og_x_peer(e))

    def x_copy(ch, i, d):
        src, dst = xs[i]
        cols = pl.ds(col_of(ch, seq_mid(d), seq_x(d)), W)
        return remote(
            src.at[:, cols], dst.at[ch, rows(j)], x_s.at[ch, i, d], x_r.at[ch, i, d], seq_peer(d)
        )

    def x_arrival(ch, i, d):
        src, dst = xs[i]
        return remote(
            src.at[:, pl.ds(0, W)], dst.at[ch, rows(seq_row(d, seq_from_x(d)))],
            x_s.at[ch, i, d], x_r.at[ch, i, d], seq_peer(d),
        )

    def x_local(ch, i):
        src, dst = xs[i]
        return pltpu.make_async_copy(
            src.at[:, pl.ds(col_of(ch, mid, jx), W)], dst.at[ch, rows(j)], x_l.at[ch, i]
        )

    def b_copy(ch, i, d):
        src, dst = bs[i]
        return remote(
            src.at[ch, rows(seq_row(d, seq_x(d)))], dst.at[:, pl.ds(col_of(ch, mid, jx), W)],
            b_s.at[ch, i, d], b_r.at[ch, i, d], seq_peer(d),
        )

    def b_arrival(ch, i, d):
        src, dst = bs[i]
        return remote(
            src.at[ch, rows(j)], dst.at[:, pl.ds(col_of(ch, seq_mid(d), seq_from_x(d)), W)],
            b_s.at[ch, i, d], b_r.at[ch, i, d], seq_peer(d),
        )

    def b_local(ch, i):
        src, dst = bs[i]
        return pltpu.make_async_copy(
            src.at[ch, rows(j)], dst.at[:, pl.ds(col_of(ch, mid, jx), W)], b_l.at[ch, i]
        )

    og_own = pltpu.make_async_copy(og_ref, og.at[rows(j)], og_l)

    def w_local(m):
        return pltpu.make_async_copy(w_rows(m), w.at[foreign + m, g], w_l.at[m])

    def g1_copy(ch):
        return remote(gs1.at[ch], gr1.at[ch], g1_s.at[ch], g1_r.at[ch], sibling)

    def g2_copy(ch, e):
        return remote(gs2.at[ch, e - 1], gr2.at[ch, e - 1], g2_s.at[ch, e], g2_r.at[ch, e], to_h(e))

    def g3_copy(n):
        source_mid, m = foreign_source(n, mid)
        return remote(
            gs3.at[n], gr3.at[m], g3_s.at[n], g3_r.at[m], (g, at(1 - u, source_mid, jx))
        )

    def g3_arrival(m):
        return remote(gr3.at[m], gr3.at[m], g3_s.at[0], g3_r.at[m], across_mid)

    @pl.when(mid == 1)
    def _():
        for m in range(O):
            w0_copy(m).start()

    og_z(0).start()
    og_z(1).start()
    for e in range(1, X):
        og_x(e).start()
    for m in range(O):
        for e in range(1, H):
            wy_copy(w_rows(m), foreign + m, e).start()
        ws_own(w_rows(m), foreign + m).start()
        w_local(m).start()
    og_own.start()

    def send_chunk(ch, carry):
        @pl.when(ch < theirs)
        def _():
            for i in range(3):
                for d in range(X, J):
                    x_copy(ch, i, d).start()

        @pl.when(ch < mine)
        def _():
            for i in range(3):
                for d in range(1, X):
                    x_copy(ch, i, d).start()
                x_local(ch, i).start()

        return carry

    for ch in range(O):
        @pl.when(mid == 0)
        def _():
            w0_copy(ch).start()

        if ch == 0:
            send_chunk(0, 0)

    def relay_w0(n):
        w0_arrival(n).wait_recv()
        for e in range(1, H):
            wy_copy(w.at[n, g], n, e).start()
        ws_own(w.at[n, g], n).start()

    def forward_w(ch):
        for e in range(1, H):
            wy_arrival(ch, e).wait_recv()
            ws_copy(ch, e).start()

    for p in range(2):
        og_z_arrival(p).wait_recv()
        for e in range(1, X):
            og_relay(e, p).start()
    lax.fori_loop(1, NM, send_chunk, 0)
    for n in range(min(2, FM)):
        @pl.when(n < foreign)
        def _():
            relay_w0(n)
    forward_w(0)
    for m in range(O):
        w_local(m).wait()
    og_own.wait()
    for e in range(1, X):
        og_x_arrival(e).wait_recv()
        og_relay_arrival(e, 0).wait_recv()
        og_relay_arrival(e, 1).wait_recv()

    seq_len = length_ref[bucket_ref[g]]
    total = count_ref[bucket_ref[0]]
    for other in range(1, G):
        total = total + count_ref[bucket_ref[other]]
    weight = jnp.full((1, 1), count_ref[bucket_ref[g]], jnp.int32).astype(F32) / jnp.full(
        (1, 1), total, jnp.int32
    ).astype(F32)
    keep_key = lax.broadcasted_iota(jnp.int32, (L, 1), 0) < seq_len
    keep_col = lax.broadcasted_iota(jnp.int32, (1, L), 1) < seq_len

    def compute(ch):
        for i in range(3):
            x_local(ch, i).wait()
            for d in range(1, J):
                x_arrival(ch, i, d).wait_recv()
        for e in range(H):
            ws_arrival(ch, e).wait_recv()
        acc = dot(og[:, 0:Dc], w[ch, 0], 1, 1)
        for gg in range(1, G):
            acc = acc + dot(og[:, gg * Dc:(gg + 1) * Dc], w[ch, gg], 1, 1)
        d_attn[...] = jnp.where(keep_key, acc, 0.0).astype(BF16)

        for n in range(W // HEAD_DIM):
            lanes = slice(n * HEAD_DIM, (n + 1) * HEAD_DIM)
            q = qh[ch, :, lanes]
            k = kh[ch, :, lanes]
            v = vh[ch, :, lanes]
            do = d_attn[:, lanes]
            scores = jnp.where(keep_key, dot(k, q, 1, 1) * scale, -1e30)
            top = jnp.max(scores, axis=0, keepdims=True)
            ex = jnp.exp(scores - top)
            probs = ex * (1.0 / jnp.sum(ex, axis=0, keepdims=True))
            low = probs.astype(BF16)
            attn = dot(v, low, 0, 0)
            attn_t[lanes, :] = jnp.where(keep_col, attn, 0.0).astype(BF16)
            dp = dot(v, do, 1, 1)
            delta = jnp.sum(probs * dp, axis=0, keepdims=True)
            ds = (probs * (dp - delta)).astype(BF16)
            dvs[ch, :, lanes] = dot(low, do, 1, 0).astype(BF16)
            dks[ch, :, lanes] = (dot(ds, q, 1, 0) * scale).astype(BF16)
            dqs[ch, :, lanes] = (dot(k, ds, 0, 0) * scale).T.astype(BF16)
        for i in range(3):
            for d in range(1, J):
                b_copy(ch, i, d).start()
            b_local(ch, i).start()

        @pl.when(ch + 1 < mine)
        def _():
            forward_w(ch + 1)

        for hh in range(H):
            low_c, high_c = (
                dot(attn_t[...], og[:, gg * Dc:(gg + 1) * Dc], 1, 0) * weight
                for gg in (2 * hh, 2 * hh + 1)
            )
            gown[ch, hh] = jnp.where(c == 0, low_c, high_c)
            gs1[ch, hh] = jnp.where(c == 0, high_c, low_c).astype(BF16)
        g1_copy(ch).start()

    def across_groups(ch):
        g1_copy(ch).wait_recv()
        for e in range(1, H):
            to = (h + e) % H
            gs2[ch, e - 1] = (gown[ch, to] + gr1[ch, to].astype(F32)).astype(BF16)
            g2_copy(ch, e).start()
        gkeep[ch] = gown[ch, h] + gr1[ch, h].astype(F32)

    def across_halves(ch):
        part = gkeep[ch]
        for e in range(1, H):
            g2_copy(ch, e).wait_recv()
            part = part + gr2[ch, e - 1].astype(F32)

        @pl.when(ch < foreign)
        def _():
            gs3[ch] = part.astype(BF16)
            g3_copy(ch).start()

        @pl.when(ch >= foreign)
        def _():
            gkeep[ch] = part

    def step(n, carry):
        @pl.when((n >= 1) & (n + 1 < foreign))
        def _():
            relay_w0(n + 1)

        @pl.when(n < mine)
        def _():
            compute(n)

        @pl.when((n >= 1) & (n < mine + 1))
        def _():
            across_groups(n - 1)

        @pl.when((n >= LAG) & (n < mine + LAG))
        def _():
            across_halves(n - LAG)

        return carry

    lax.fori_loop(0, mine + LAG, step, 0)

    for m in range(O):
        g3_arrival(m).wait_recv()
        gw_ref[m * W:(m + 1) * W, :] = gkeep[foreign + m] + gr3[m].astype(F32)

    og_z(0).wait_send()
    og_z(1).wait_send()
    for e in range(1, X):
        og_x(e).wait_send()
        og_relay(e, 0).wait_send()
        og_relay(e, 1).wait_send()
    for m in range(O):
        w0_copy(m).wait_send()

    def drain(ch, carry):
        @pl.when(ch < foreign)
        def _():
            g3_copy(ch).wait_send()

        @pl.when(ch < mine)
        def _():
            ws_own(w.at[ch, g], ch).wait_send()
            for e in range(1, H):
                ws_copy(ch, e).wait_send()
                wy_copy(w.at[ch, g], ch, e).wait_send()
                g2_copy(ch, e).wait_send()
            g1_copy(ch).wait_send()
            for i in range(3):
                b_local(ch, i).wait()
                for d in range(1, J):
                    b_copy(ch, i, d).wait_send()
                for d in range(1, X):
                    x_copy(ch, i, d).wait_send()
                    b_arrival(ch, i, d).wait_recv()

        @pl.when(ch < theirs)
        def _():
            for i in range(3):
                for d in range(X, J):
                    x_copy(ch, i, d).wait_send()
                    b_arrival(ch, i, d).wait_recv()

        return carry

    lax.fori_loop(0, NM, drain, 0)


def solution(mesh):
    G, S = mesh.shape["grp"], mesh.shape["sp"]
    J, H = S // SEQS, G // 2
    X = J // 2

    def shards(bucket_of, lengths, counts, queries, keys, values, out_grad, w_out):
        T, HD = queries.shape
        D = out_grad.shape[1]
        L, R, Dc = J * T, HD // S, D // G
        W = 256 if R % 256 == 0 else 128
        O = R // W
        E = O // 2
        NM = 3 * O - E
        FM = NM - O
        dma = pltpu.SemaphoreType.DMA
        head = pltpu.VMEM((NM, L, W), BF16)
        smem = pl.BlockSpec(memory_space=pltpu.SMEM)
        hbm = pl.BlockSpec(memory_space=pltpu.HBM)
        grad = jax.ShapeDtypeStruct((T, HD), BF16)
        return pl.pallas_call(
            functools.partial(kernel, G, S, D, W, E),
            out_shape=(grad, grad, grad, jax.ShapeDtypeStruct((R, Dc), F32)),
            in_specs=[smem] * 3 + [hbm] * 5,
            out_specs=(hbm, hbm, hbm, pl.BlockSpec(memory_space=pltpu.VMEM)),
            scratch_shapes=[head] * 6 + [
                pltpu.VMEM((L, D), BF16),
                pltpu.VMEM((NM, G, W, Dc), BF16),
                pltpu.VMEM((L, W), BF16),
                pltpu.VMEM((W, L), BF16),
                pltpu.VMEM((NM, H, W, Dc), BF16),
                pltpu.VMEM((NM, H, W, Dc), BF16),
                pltpu.VMEM((NM, H, W, Dc), F32),
                pltpu.VMEM((NM, H - 1, W, Dc), BF16),
                pltpu.VMEM((NM, H - 1, W, Dc), BF16),
                pltpu.VMEM((NM, W, Dc), F32),
                pltpu.VMEM((FM, W, Dc), BF16),
                pltpu.VMEM((O, W, Dc), BF16),
                dma((X,)), dma((X,)), dma((2,)), dma((2,)), dma((X, 2)), dma((X, 2)), dma(()),
                dma((NM, 3, J)), dma((NM, 3, J)), dma((NM, 3)),
                dma((NM, 3, J)), dma((NM, 3, J)), dma((NM, 3)),
                dma((O,)), dma((FM,)), dma((O,)),
                dma((NM, H)), dma((NM, H)), dma((NM, H)), dma((NM, H)),
                dma((NM,)), dma((NM,)), dma((NM, H)), dma((NM, H)),
                dma((FM,)), dma((O,)),
            ],
            compiler_params=pltpu.CompilerParams(
                collective_id=0, has_side_effects=True, vmem_limit_bytes=62 * 1024 * 1024
            ),
        )(bucket_of, lengths, counts, queries, keys, values, out_grad, w_out)

    rows = P(("grp", "sp"), None)
    return jax.shard_map(
        shards,
        mesh=mesh,
        in_specs=(P(), P(), P(), rows, rows, rows, rows, P("sp", "grp")),
        out_specs=(rows, rows, rows, P("sp", "grp")),
        check_vma=False,
    )
```

time: 135 us -> 129 us (0.956)
  Pallas kernels: 129 us -> 123 us
    pallas_call x1, Pallas kernels: 129 us -> 123 us  [shards(): pl.pallas_call(functools.partial(kernel, G, S, D, W, E), out_shape=(grad,...]
where the time goes in v1:
time: 129 us
  Pallas kernels  123 us (95%)
  local copies, waits for them, and re-layouts  5.53 us (4%)
    pallas_call x1, Pallas kernels, shards(): pl.pallas_call(functools.partial(kernel, G, S, D, W, E), out_shape=(grad,...  123 us
    unnamed x10, local copies, waits for them, and re-layouts  5.53 us

profile of v1, /device:TPU:0, one launch (start us, length us, event | category | flops | bytes accessed | tf_op | source)
XLA Modules:
  0.0 129.0 jit_solution(1544507110962764256)
XLA Ops:
  0.6 122.8 %shard_map.111 = (bf16[128,4096]{1,0:T(8,128)(2,1)}, bf16[128,4096]{1,0:T(8,128)(2,1)}, bf16[128,4096]{1,0:T(8,128)(2,1)}, f32[512,768]{1,0:T(8,128)}) custom-call(s32[4]{0:T(128)} %bucket_ref.1, s32[4]{0:T(128)} %length_ref.1, s32[4]{0:T(128)} %count_ref.1, bf16[128,4096]{1,0:T(8,128)(2,1)} %q_ref.1, bf16[128,4096]{1,0:T(8,128)(2,1)} %k_ref.1, ...), custom_call_target="tpu_custom_call" | custom-call | tf_op jit(solution)/shard_map/pallas_call | solution.py:474
  123.5 0.0 copy-start.2
  123.5 0.0 copy-start.1
  123.5 2.4 %copy.16 = bf16[128,4096]{1,0:T(8,128)(2,1)} copy(bf16[128,4096]{1,0:T(8,128)(2,1)} %get-tuple-element.8) | data formatting | bytes 2097152
  125.9 0.0 copy-done.2
  125.9 0.0 copy-start
  125.9 1.0 copy.17
  126.9 0.0 copy-done.1
  126.9 1.0 copy.18
  127.9 0.0 copy-done
  127.9 1.1 copy.19
Async XLA Ops:
  123.5 2.5 %copy-start.2 = (bf16[128,4096]{1,0:T(8,128)(2,1)S(1)}, bf16[128,4096]{1,0:T(8,128)(2,1)}, u32[]{:S(2)}) copy-start(bf16[128,4096]{1,0:T(8,128)(2,1)} %get-tuple-element.9) | copy-start | bytes 3145732
  123.5 3.4 %copy-start.1 = (bf16[128,4096]{1,0:T(8,128)(2,1)S(1)}, bf16[128,4096]{1,0:T(8,128)(2,1)}, u32[]{:S(2)}) copy-start(bf16[128,4096]{1,0:T(8,128)(2,1)} %get-tuple-element.10) | copy-start | bytes 3145732
  125.9 1.9 %copy-start = (f32[512,768]{1,0:T(8,128)S(1)}, f32[512,768]{1,0:T(8,128)}, u32[]{:S(2)}) copy-start(f32[512,768]{1,0:T(8,128)} %get-tuple-element.11) | copy-start | bytes 4718596

commit v2 on v1

--- a/solution.py
+++ b/solution.py
@@ -10,6 +10,7 @@
 HEAD_DIM = 128
 SEQS = 2
 LAG = 2
+PARTS = 2
 MESH = pl.DeviceIdType.MESH
 F32 = jnp.float32
 BF16 = jnp.bfloat16
@@ -17,6 +18,19 @@
 
 def dot(a, b, ca, cb):
     return lax.dot_general(a, b, (((ca,), (cb,)), ((), ())), preferred_element_type=F32)
+
+
+def schedule(role, O, E, NM):
+    w0 = [("w0", m) for m in range(O)]
+    if role == 1:
+        w0 = w0[E:] + w0[:E]
+    first = [("ogz", 0), ("ogz", 1), ("ogx", 0), ("wy", 0)]
+    relays = [("ogr", 0), ("ogr", 1)]
+    last = [("relay", 0), ("relay", 1), ("fwd", 0)]
+    rest = [(kind, ch) for ch in range(1, NM) for kind in ("x1", "x3", "x2")]
+    if role == 0:
+        return first + w0[:1] + [("x1", 0), ("x3", 0), ("x2", 0)] + w0[1:] + relays + rest + last
+    return w0 + first + [("x1", 0), ("x3", 0), ("x2", 0)] + relays + rest + last
 
 
 def kernel(
@@ -94,8 +108,6 @@
     def _():
         pl.semaphore_signal(barrier, inc=1, device_id=across_edge, device_id_type=MESH)
 
-    pl.semaphore_wait(barrier, len(peers) + mid)
-
     def remote(src, dst, ss, rs, dev):
         return pltpu.make_async_remote_copy(
             src_ref=src, dst_ref=dst, send_sem=ss, recv_sem=rs, device_id=dev, device_id_type=MESH
@@ -234,45 +246,17 @@
     def g3_arrival(m):
         return remote(gr3.at[m], gr3.at[m], g3_s.at[0], g3_r.at[m], across_mid)
 
-    @pl.when(mid == 1)
-    def _():
-        for m in range(O):
-            w0_copy(m).start()
-
-    og_z(0).start()
-    og_z(1).start()
-    for e in range(1, X):
-        og_x(e).start()
+    og_own.start()
     for m in range(O):
-        for e in range(1, H):
-            wy_copy(w_rows(m), foreign + m, e).start()
-        ws_own(w_rows(m), foreign + m).start()
         w_local(m).start()
-    og_own.start()
-
-    def send_chunk(ch, carry):
-        @pl.when(ch < theirs)
-        def _():
-            for i in range(3):
-                for d in range(X, J):
-                    x_copy(ch, i, d).start()
-
-        @pl.when(ch < mine)
-        def _():
-            for i in range(3):
-                for d in range(1, X):
-                    x_copy(ch, i, d).start()
-                x_local(ch, i).start()
-
+
+    def local_chunk(ch, carry):
+        for i in range(3):
+            x_local(ch, i).start()
         return carry
 
-    for ch in range(O):
-        @pl.when(mid == 0)
-        def _():
-            w0_copy(ch).start()
-
-        if ch == 0:
-            send_chunk(0, 0)
+    lax.fori_loop(0, mine, local_chunk, 0)
+    pl.semaphore_wait(barrier, len(peers) + mid)
 
     def relay_w0(n):
         w0_arrival(n).wait_recv()
@@ -285,16 +269,48 @@
             wy_arrival(ch, e).wait_recv()
             ws_copy(ch, e).start()
 
-    for p in range(2):
-        og_z_arrival(p).wait_recv()
-        for e in range(1, X):
-            og_relay(e, p).start()
-    lax.fori_loop(1, NM, send_chunk, 0)
-    for n in range(min(2, FM)):
-        @pl.when(n < foreign)
-        def _():
+    def issue(kind, n, role):
+        theirs_n = E + (1 - role) * (FM - E) + O
+        mine_n = E + role * (FM - E) + O
+        first = mine_n - O
+        if kind == "w0" and n < O:
+            w0_copy(n).start()
+        elif kind == "ogz":
+            og_z(n).start()
+        elif kind == "ogx":
+            for e in range(1, X):
+                og_x(e).start()
+        elif kind == "ogr":
+            og_z_arrival(n).wait_recv()
+            for e in range(1, X):
+                og_relay(e, n).start()
+        elif kind == "wy":
+            for m in range(O):
+                for e in range(1, H):
+                    wy_copy(w_rows(m), first + m, e).start()
+                ws_own(w_rows(m), first + m).start()
+        elif kind == "x1" and n < theirs_n:
+            for i in range(3):
+                x_copy(n, i, X).start()
+        elif kind == "x3" and n < theirs_n:
+            for i in range(3):
+                for d in range(X + 1, J):
+                    x_copy(n, i, d).start()
+        elif kind == "x2" and n < mine_n:
+            for i in range(3):
+                for d in range(1, X):
+                    x_copy(n, i, d).start()
+        elif kind == "relay" and n < first:
             relay_w0(n)
-    forward_w(0)
+        elif kind == "fwd":
+            forward_w(n)
+
+    for role in range(2):
+        @pl.when(mid == role)
+        def _():
+            for kind, n in schedule(role, O, E, NM):
+                issue(kind, n, role)
+
     for m in range(O):
         w_local(m).wait()
     og_own.wait()
@@ -324,6 +340,10 @@
         for gg in range(1, G):
             acc = acc + dot(og[:, gg * Dc:(gg + 1) * Dc], w[ch, gg], 1, 1)
         d_attn[...] = jnp.where(keep_key, acc, 0.0).astype(BF16)
+
+        @pl.when(ch >= 1)
+        def _():
+            across_groups(ch - 1)
 
         for n in range(W // HEAD_DIM):
             lanes = slice(n * HEAD_DIM, (n + 1) * HEAD_DIM)
@@ -353,6 +373,10 @@
         def _():
             forward_w(ch + 1)
 
+        @pl.when(ch >= LAG)
+        def _():
+            across_halves(ch - LAG)
+
         for hh in range(H):
             low_c, high_c = (
                 dot(attn_t[...], og[:, gg * Dc:(gg + 1) * Dc], 1, 0) * weight
@@ -390,21 +414,15 @@
         def _():
             relay_w0(n + 1)
 
-        @pl.when(n < mine)
-        def _():
-            compute(n)
-
-        @pl.when((n >= 1) & (n < mine + 1))
-        def _():
-            across_groups(n - 1)
-
-        @pl.when((n >= LAG) & (n < mine + LAG))
-        def _():
-            across_halves(n - LAG)
-
+        compute(n)
         return carry
 
-    lax.fori_loop(0, mine + LAG, step, 0)
+    lax.fori_loop(0, mine, step, 0)
+    across_groups(mine - 1)
+    for n in range(LAG, 0, -1):
+        @pl.when(mine >= n)
+        def _():
+            across_halves(mine - n)
 
     for m in range(O):
         g3_arrival(m).wait_recv()
@@ -450,6 +468,20 @@
         return carry
 
     lax.fori_loop(0, NM, drain, 0)
+
+
+def store(*refs):
+    sems = refs[-1]
+    copies = []
+    for i in range(4):
+        rows = refs[i].shape[0] // PARTS
+        for n in range(PARTS):
+            part = pl.ds(n * rows, rows)
+            copies.append(pltpu.make_async_copy(refs[i].at[part], refs[4 + i].at[part], sems.at[i, n]))
+    for copy in copies:
+        copy.start()
+    for copy in copies:
+        copy.wait()
 
 
 def solution(mesh):
@@ -471,11 +503,11 @@
         smem = pl.BlockSpec(memory_space=pltpu.SMEM)
         hbm = pl.BlockSpec(memory_space=pltpu.HBM)
         grad = jax.ShapeDtypeStruct((T, HD), BF16)
-        return pl.pallas_call(
+        held = pl.pallas_call(
             functools.partial(kernel, G, S, D, W, E),
-            out_shape=(grad, grad, grad, jax.ShapeDtypeStruct((R, Dc), F32)),
+            out_shape=(pltpu.VMEM((T, HD), BF16),) * 3 + (pltpu.VMEM((R, Dc), F32),),
             in_specs=[smem] * 3 + [hbm] * 5,
-            out_specs=(hbm, hbm, hbm, pl.BlockSpec(memory_space=pltpu.VMEM)),
+            out_specs=(pl.BlockSpec(memory_space=pltpu.VMEM),) * 4,
             scratch_shapes=[head] * 6 + [
                 pltpu.VMEM((L, D), BF16),
                 pltpu.VMEM((NM, G, W, Dc), BF16),
@@ -498,9 +530,18 @@
                 dma((FM,)), dma((O,)),
             ],
             compiler_params=pltpu.CompilerParams(
-                collective_id=0, has_side_effects=True, vmem_limit_bytes=62 * 1024 * 1024
+                collective_id=0, has_side_effects=True, vmem_limit_bytes=56 * 1024 * 1024
             ),
         )(bucket_of, lengths, counts, queries, keys, values, out_grad, w_out)
+        vmem = pl.BlockSpec(memory_space=pltpu.VMEM)
+        return pl.pallas_call(
+            store,
+            out_shape=(grad, grad, grad, jax.ShapeDtypeStruct((R, Dc), F32)),
+            in_specs=[vmem] * 4,
+            out_specs=(hbm,) * 4,
+            scratch_shapes=[dma((4, PARTS))],
+            compiler_params=pltpu.CompilerParams(vmem_limit_bytes=1024 * 1024),
+        )(*held)
 
     rows = P(("grp", "sp"), None)
     return jax.shard_map(

time: 129 us -> 126 us (0.977)
  local copies, waits for them, and re-layouts: 5.53 us -> 0 us
  Pallas kernels: 123 us -> 125 us
    unnamed x10 -> x0, local copies, waits for them, and re-layouts: 5.53 us -> none
    pallas_call x1 -> x2, Pallas kernels: 123 us -> 125 us  [the longest x1 123 us: shards(): pl.pallas_call(functools.partial(kernel, G, S, D, W, E), out_shape=(pltpu...]
where the time goes in v2:
time: 126 us
  Pallas kernels  125 us (99%)
    pallas_call x1, Pallas kernels, shards(): pl.pallas_call(functools.partial(kernel, G, S, D, W, E), out_shape=(pltpu...  123 us

profile of v2, /device:TPU:0, one launch (start us, length us, event | category | flops | bytes accessed | tf_op | source)
XLA Modules:
  0.0 125.6 jit_solution(8575164992353737606)
XLA Ops:
  0.6 122.7 %shard_map.111 = (bf16[128,4096]{1,0:T(8,128)(2,1)S(1)}, bf16[128,4096]{1,0:T(8,128)(2,1)S(1)}, bf16[128,4096]{1,0:T(8,128)(2,1)S(1)}, f32[512,768]{1,0:T(8,128)S(1)}) custom-call(s32[4]{0:T(128)} %bucket_ref.1, s32[4]{0:T(128)} %length_ref.1, s32[4]{0:T(128)} %count_ref.1, bf16[128,4096]{1,0:T(8,128)(2,1)} %q_ref.1, bf16[128,4096]{1,0:T(8,128)(2,1)} %k_ref.1, ...), custom_call_target="tpu_custom_call" | custom-call | tf_op jit(solution)/shard_map/pallas_call | solution.py:506
  123.3 2.2 %shard_map.112 = (bf16[128,4096]{1,0:T(8,128)(2,1)}, bf16[128,4096]{1,0:T(8,128)(2,1)}, bf16[128,4096]{1,0:T(8,128)(2,1)}, f32[512,768]{1,0:T(8,128)}) custom-call(bf16[128,4096]{1,0:T(8,128)(2,1)S(1)} %get-tuple-element.8.refs_0_, bf16[128,4096]{1,0:T(8,128)(2,1)S(1)} %get-tuple-element.9.refs_1_, bf16[128,4096]{1,0:T(8,128)(2,1)S(1)} %get-tuple-element.10.refs_2_, ...), custom_call_target="tpu_custom_call" | custom-call | tf_op jit(solution)/shard_map/pallas_call | solution.py:537

commit v3 on v2

--- a/solution.py
+++ b/solution.py
@@ -20,17 +20,28 @@
     return lax.dot_general(a, b, (((ca,), (cb,)), ((), ())), preferred_element_type=F32)
 
 
+END_ORDER = (
+    ("x3", 0), ("ogz", 0), ("ogz", 1), ("w0", 0), ("w0", 1), ("ogx", 0), ("x1", 0), ("x3", 1),
+    ("x1", 1), ("wy", 0), ("x3", 2), ("x1", 2), ("x2", 1), ("relay", 0), ("x3", 3), ("x2", 0),
+    ("ogr", 1), ("x1", 3), ("x3", 4), ("fwd", 0), ("ogr", 0), ("x2", 2), ("x1", 4),
+)
+MIDDLE_ORDER = (
+    ("wy", 0), ("x3", 1), ("x3", 2), ("ogz", 1), ("x1", 0), ("x3", 0), ("w0", 1), ("w0", 0),
+    ("x2", 0), ("ogx", 0), ("ogr", 0), ("ogr", 1), ("relay", 0), ("x2", 1), ("fwd", 0), ("x2", 2),
+    ("relay", 1), ("ogz", 0), ("x2", 3), ("x2", 4), ("x1", 2), ("x1", 1), ("relay", 2),
+)
+
+
 def schedule(role, O, E, NM):
+    if (O, E) == (2, 1):
+        return MIDDLE_ORDER if role == 1 else END_ORDER
     w0 = [("w0", m) for m in range(O)]
-    if role == 1:
-        w0 = w0[E:] + w0[:E]
-    first = [("ogz", 0), ("ogz", 1), ("ogx", 0), ("wy", 0)]
-    relays = [("ogr", 0), ("ogr", 1)]
-    last = [("relay", 0), ("relay", 1), ("fwd", 0)]
-    rest = [(kind, ch) for ch in range(1, NM) for kind in ("x1", "x3", "x2")]
-    if role == 0:
-        return first + w0[:1] + [("x1", 0), ("x3", 0), ("x2", 0)] + w0[1:] + relays + rest + last
-    return w0 + first + [("x1", 0), ("x3", 0), ("x2", 0)] + relays + rest + last
+    start = [("ogz", 0), ("ogz", 1), ("ogx", 0), ("wy", 0)]
+    og_relays = [("ogr", 0), ("ogr", 1)]
+    chunks = [(kind, ch) for ch in range(1, NM) for kind in ("x1", "x3", "x2")]
+    w_relays = [("relay", 0), ("fwd", 0)] + [("relay", n) for n in range(1, NM - O)]
+    first = [("x1", 0), ("x3", 0), ("x2", 0)] + og_relays + chunks + w_relays
+    return start + w0 + first if role == 0 else w0[E:] + w0[:E] + start + first
 
 
 def kernel(
@@ -364,9 +375,21 @@
             dvs[ch, :, lanes] = dot(low, do, 1, 0).astype(BF16)
             dks[ch, :, lanes] = (dot(ds, q, 1, 0) * scale).astype(BF16)
             dqs[ch, :, lanes] = (dot(k, ds, 0, 0) * scale).T.astype(BF16)
+
+        def send_back(ds):
+            for d in ds:
+                for i in range(3):
+                    b_copy(ch, i, d).start()
+
+        @pl.when(mid == 0)
+        def _():
+            send_back(range(1, J))
+
+        @pl.when(mid == 1)
+        def _():
+            send_back(list(range(X + 1, J)) + list(range(1, X)) + [X])
+
         for i in range(3):
-            for d in range(1, J):
-                b_copy(ch, i, d).start()
             b_local(ch, i).start()
 
         @pl.when(ch + 1 < mine)
@@ -410,10 +433,6 @@
             gkeep[ch] = part
 
     def step(n, carry):
-        @pl.when((n >= 1) & (n + 1 < foreign))
-        def _():
-            relay_w0(n + 1)
-
         compute(n)
         return carry
 

time: 126 us -> 123 us (0.976)
  Pallas kernels: 125 us -> 122 us
    pallas_call x1, Pallas kernels: 123 us -> 120 us  [shards(): pl.pallas_call(functools.partial(kernel, G, S, D, W, E), out_shape=(pltpu...]
where the time goes in v3:
time: 123 us
  Pallas kernels  122 us (99%)
    pallas_call x1, Pallas kernels, shards(): pl.pallas_call(functools.partial(kernel, G, S, D, W, E), out_shape=(pltpu...  120 us

profile of v3, /device:TPU:0, one launch (start us, length us, event | category | flops | bytes accessed | tf_op | source)
XLA Modules:
  0.0 123.0 jit_solution(7963317927318928306)
XLA Ops:
  0.6 120.1 %shard_map.111 = (bf16[128,4096]{1,0:T(8,128)(2,1)S(1)}, bf16[128,4096]{1,0:T(8,128)(2,1)S(1)}, bf16[128,4096]{1,0:T(8,128)(2,1)S(1)}, f32[512,768]{1,0:T(8,128)S(1)}) custom-call(s32[4]{0:T(128)} %bucket_ref.1, s32[4]{0:T(128)} %length_ref.1, s32[4]{0:T(128)} %count_ref.1, bf16[128,4096]{1,0:T(8,128)(2,1)} %q_ref.1, bf16[128,4096]{1,0:T(8,128)(2,1)} %k_ref.1, ...), custom_call_target="tpu_custom_call" | custom-call | tf_op jit(solution)/shard_map/pallas_call | solution.py:525
  120.8 2.2 %shard_map.112 = (bf16[128,4096]{1,0:T(8,128)(2,1)}, bf16[128,4096]{1,0:T(8,128)(2,1)}, bf16[128,4096]{1,0:T(8,128)(2,1)}, f32[512,768]{1,0:T(8,128)}) custom-call(bf16[128,4096]{1,0:T(8,128)(2,1)S(1)} %get-tuple-element.8.refs_0_, bf16[128,4096]{1,0:T(8,128)(2,1)S(1)} %get-tuple-element.9.refs_1_, bf16[128,4096]{1,0:T(8,128)(2,1)S(1)} %get-tuple-element.10.refs_2_, ...), custom_call_target="tpu_custom_call" | custom-call | tf_op jit(solution)/shard_map/pallas_call | solution.py:556
